TPU v7x, 256 devices: a whole 4x4x8 slice. The times are simulated.
256 devices in a mesh: prow: 16 (over z, core), pcol: 16 (over x, y).
Axes of the slice: x: 4, y: 4, z: 8, core: 2. Of those that a mesh axis runs over, the one named last changes fastest.
Arguments:
- inv_lead: float32 [4, 16, 256, 4, 16, 256], P(None, 'prow', None, None, 'pcol'), may hold values from -1 to 2, as said below
- h_lead: float32 [4, 16, 256, 6, 16, 256], P(None, 'pcol', None, None, 'prow'), may hold values from -6 to 6
- h_slab: float32 [512, 6, 16, 256], P('pcol', None, 'prow'), may hold values from -6 to 6
- l_panel: float32 [512, 4, 16, 256], P('pcol', None, 'prow'), may hold values from -0.046875 to 0.046875
- l_diag: float32 [512, 512], replicated, may hold values from -1 to 2, as said below
Outputs:
- x_slab: float32 [512, 6, 16, 256], P('pcol', None, 'prow')
- y_lead: float32 [512, 4, 16, 256], P('pcol', None, 'prow')
- y_diag: float32 [512, 512], P('pcol', 'prow')
Inputs may be any that keep to these rules, and one draw needn't show every extreme that they name: inv_lead is lower triangular in natural order, with diagonal entries between 1 and 2. l_diag is lower triangular, with diagonal entries between 1 and 2.
All inputs are finite; a program needn't handle non-finite values.
Results may differ from a plain program's by a relative error of at most 0.00018.
Values sent between devices are 32-bit elements; how exact they have to be, the bound alone decides.
No kernel may reach another device: no remote copies, remote signals or barrier semaphores. Data moves between devices by JAX's collectives and lax.ppermute only.
A program may use at most 128 MiB of HBM per device.

v0:
```python
import jax
import jax.numpy as jnp
from jax import lax
from jax.sharding import PartitionSpec as P


def copy_for_each(value, axis):
    copies = jnp.broadcast_to(value, (lax.axis_size(axis), *value.shape))
    return lax.all_to_all(copies, axis, split_axis=0, concat_axis=0, tiled=True)


def joined_along(parts, dim):
    lengths = list(parts.shape[1:])
    lengths[dim] *= parts.shape[0]
    return jnp.moveaxis(parts, 0, dim).reshape(lengths)


def gathered_copies(value, axis, dim):
    parts = copy_for_each(value, axis)
    return joined_along(parts, dim)


def in_blocks(value, dim, size):
    lengths = value.shape
    parts = value.reshape(*lengths[:dim], size, lengths[dim] // size, *lengths[dim + 1 :])
    return jnp.moveaxis(parts, dim, 0)


def sum_at_owner(value, axis, dim):
    parts = in_blocks(value, dim, lax.axis_size(axis))
    arrived = lax.all_to_all(parts, axis, split_axis=0, concat_axis=0, tiled=True)
    return arrived.sum(axis=0)


def in_one_piece(arrays, axis, dim, along):
    widths = [a.shape[along] for a in arrays]
    both = jnp.concatenate(arrays, axis=along)
    result = lax.psum_scatter(both, axis, scatter_dimension=dim, tiled=True)
    return tuple(jnp.split(result, [sum(widths[:k]) for k in range(1, len(widths))], axis=along))


def matmul_hi(left, right):
    return jnp.dot(left, right, precision=lax.Precision.HIGHEST, preferred_element_type=jnp.float32)


def matmul_trans(left, right):
    return lax.dot_general(
        left,
        right,
        (((1,), (1,)), ((), ())),
        precision=lax.Precision.HIGHEST,
        preferred_element_type=jnp.float32,
    )


def invert_diag(l_diag, block_size):
    diag_top = l_diag[:block_size, :block_size]
    diag_bottom = l_diag[block_size:, block_size:]
    off_block = l_diag[block_size:, :block_size]
    identity = jnp.eye(block_size, dtype=jnp.float32)
    top_inv = lax.linalg.triangular_solve(diag_top, identity, left_side=True, lower=True)
    bottom_inv = lax.linalg.triangular_solve(diag_bottom, identity, left_side=True, lower=True)
    corner = -matmul_hi(bottom_inv, matmul_hi(off_block, top_inv))
    upper_rows = jnp.concatenate([top_inv, jnp.zeros_like(top_inv)], axis=1)
    lower_rows = jnp.concatenate([corner, bottom_inv], axis=1)
    return jnp.concatenate([upper_rows, lower_rows], axis=0)


def per_device(inv_lead, h_lead, h_slab, l_panel, l_diag):
    slab_rows = l_diag.shape[0]
    block_size = l_panel.shape[3]
    prev_blocks = l_panel.shape[1]
    x_rows = l_panel.shape[0]
    h_blocks = h_slab.shape[1]
    diag_inv = invert_diag(l_diag, slab_rows // 2)
    inv_local = inv_lead.reshape(prev_blocks * block_size, -1)
    col_width = inv_local.shape[1]
    col_blocks = col_width // block_size
    h_local = h_lead.reshape(col_width, -1)
    h_side = h_slab.reshape(x_rows, -1)
    y_rows = slab_rows // lax.axis_size("prow")
    row_start = lax.axis_index("prow") * y_rows
    col_start = lax.axis_index("pcol") * x_rows
    piece = gathered_copies(l_panel, "pcol", 0)
    factor = matmul_hi(diag_inv, piece.reshape(piece.shape[0], -1))
    side_term = matmul_hi(lax.dynamic_slice_in_dim(diag_inv, col_start, x_rows, 1), h_side)
    own_panel = sum_at_owner(-matmul_hi(factor, inv_local), "prow", 0)
    product = matmul_hi(lax.all_gather(own_panel, "prow", axis=0, tiled=True), h_local)
    x_local = sum_at_owner(product + side_term, "pcol", 0)
    x_slab = x_local.reshape(x_rows, h_blocks, 1, block_size)
    kept_cols = x_slab[:, : prev_blocks + 1]
    widened = lax.all_gather(kept_cols, "prow", axis=2, tiled=True).reshape(x_rows, -1)
    prev_rows = prev_blocks * block_size * lax.axis_size("prow")
    head_cols = widened[:, :prev_rows]
    tail_cols = widened[:, prev_rows : prev_rows + slab_rows]
    shifted_x = lax.all_to_all(
        head_cols.reshape(x_rows, col_blocks, lax.axis_size("pcol"), block_size),
        "pcol",
        split_axis=2,
        concat_axis=0,
        tiled=True,
    )
    shifted_x = shifted_x.reshape(slab_rows, col_width)
    lead_part = matmul_trans(shifted_x, inv_local)
    diag_part = matmul_trans(shifted_x, own_panel)
    y_first, y_block = in_one_piece((lead_part, diag_part), "pcol", 0, 1)
    diag_rows = lax.dynamic_slice_in_dim(diag_inv, row_start, y_rows, 0)
    y_diag = y_block + matmul_trans(tail_cols, diag_rows)
    return (x_slab, y_first.reshape(x_rows, prev_blocks, 1, block_size), y_diag)


def solution(mesh):
    return jax.shard_map(
        per_device,
        mesh=mesh,
        in_specs=(
            P(None, "prow", None, None, "pcol", None),
            P(None, "pcol", None, None, "prow", None),
            P("pcol", None, "prow", None),
            P("pcol", None, "prow", None),
            P(),
        ),
        out_specs=(P("pcol", None, "prow", None), P("pcol", None, "prow", None), P("pcol", "prow")),
        check_vma=False,
    )
```

profile of v0, /device:TPU:2, one launch (start us, length us, event | category | flops | bytes accessed | tf_op | source)
XLA Modules:
  0.0 457.1 jit_solution(1383191247335577584)
XLA Ops:
  8.1 2.9 broadcast_in_dim.4
  11.1 7.5 %all-to-all-start = ((f32[16,32,4,1,256]{4,3,2,1,0:T(1,128)}), f32[16,32,4,1,256]{4,3,2,1,0:T(1,128)S(1)}, u32[]{:S(2)}, u32[]{:S(2)}) async-start(f32[16,32,4,1,256]{4,3,2,1,0:T(1,128)} %broadcast_in_dim.4), calls=%async_computation | async-start | bytes 4194304 | tf_op jit(solution)/shard_map/all_to_all | solution.py:9
  19.8 3.8 while.4
  23.6 19.7 %custom-call.4 = f32[2,128,128]{1,2,0:T(8,128)S(1)} custom-call(f32[2,128,128]{2,1,0:T(8,128)S(1)} %get-tuple-element.18), custom_call_target="InvertDiagBlocksLowerTriangular" | custom-call | tf_op jit(solution)/shard_map/triangular_solve/custom-call.1 | solution.py:61
  43.3 4.0 while.5
  43.9 1.4 bitcast_dynamic-update-slice_fusion.5
  45.9 1.4 bitcast_dynamic-update-slice_fusion.5
  47.3 19.7 %custom-call.5 = f32[2,128,128]{1,2,0:T(8,128)S(1)} custom-call(f32[2,128,128]{2,1,0:T(8,128)S(1)} %get-tuple-element.19), custom_call_target="InvertDiagBlocksLowerTriangular" | custom-call | tf_op jit(solution)/shard_map/triangular_solve/custom-call.1 | solution.py:62
  67.0 14.2 %reduce.1 = f32[4,256,4,256]{3,2,1,0:T(4,128)} reduce(f32[4,1,256,4,1,256]{5,4,3,2,1,0:T(1,128)} %param.7, f32[]{:T(128)} %constant.47), dimensions={1,4}, to_apply=%param.7.reduce_sub_computation | reduce | bytes 8388612 | tf_op args[0]
  81.2 5.2 %copy.34 = f32[128,8,4,256]{3,1,2,0:T(8,128)} copy(f32[128,8,4,256]{3,2,1,0:T(4,128)} %bitcast.82) | data formatting | bytes 8388608
  88.2 1.5 fusion.6
  90.2 7.4 %reduce = f32[16,32,4,256]{3,2,1,0:T(4,128)} reduce(f32[16,32,4,1,256]{4,3,2,1,0:T(1,128)S(1)} %all-to-all-done, f32[]{:T(128)} %constant.47), dimensions={3}, to_apply=%all_to_all.20.reduce_sub_computation | reduce | bytes 4194308 | tf_op jit(solution)/shard_map/all_to_all | solution.py:9
  97.6 2.1 copy.33
  99.7 4.0 fusion.22
  103.7 6.9 %convolution_negate_fusion = f32[512,1024]{1,0:T(8,128)S(1)} fusion(f32[512,1024]{1,0:T(8,128)S(1)} %fusion.22, f32[1024,1024]{1,0:T(8,128)S(1)} %bitcast.77), kind=kOutput, calls=%fused_computation.6 | convolution fusion | flops 6442975232 | bytes 8388608 | tf_op jit(solution)/shard_map/dot_general | solution.py:43
  110.6 58.0 %all_to_all.31 = f32[16,32,1024]{2,1,0:T(8,128)S(1)} all-to-all(f32[16,32,1024]{2,1,0:T(8,128)S(1)} %bitcast.92), channel_id=1, replica_groups=mesh['prow'=16,'pcol'=16] {'prow'}, dimensions={0} | all-to-all | bytes 4194304 | tf_op jit(solution)/shard_map/all_to_all | solution.py:31
  169.5 37.4 %reduce.2 = f32[4,256,6,256]{3,2,1,0:T(8,128)} reduce(f32[4,1,256,6,1,256]{5,4,3,2,1,0:T(1,128)} %param.8, f32[]{:T(128)} %constant.47), dimensions={1,4}, to_apply=%param.8.reduce_sub_computation | reduce | bytes 12582916 | tf_op args[1]
  206.8 9.2 %copy.35 = f32[128,8,6,256]{3,1,2,0:T(8,128)} copy(f32[128,8,6,256]{3,2,1,0:T(8,128)} %bitcast.79) | data formatting | bytes 12582912
  216.8 13.7 %fusion.25 = f32[512,1536]{1,0:T(8,128)S(1)} fusion(f32[512,1024]{1,0:T(8,128)} %all-gather.3.cloned.1.call-done, f32[1024,1536]{1,0:T(8,128)} %bitcast.93), kind=kOutput, calls=%fused_computation.47 | convolution fusion | flops 9663676416 | bytes 11534336 | tf_op jit(solution)/shard_map/dot_general | solution.py:43
  230.4 2.8 convolution_add_fusion
  233.2 45.1 %all_to_all.32 = f32[16,32,1536]{2,1,0:T(8,128)S(1)} all-to-all(f32[16,32,1536]{2,1,0:T(8,128)S(1)} %bitcast.83), channel_id=1, replica_groups=mesh['prow'=16,'pcol'=16] {'pcol'}, dimensions={0} | all-to-all | bytes 6291456 | tf_op jit(solution)/shard_map/all_to_all | solution.py:31
  279.4 36.6 %all-gather.5.cloned.1.call-done = f32[32,5,16,256]{3,0,1,2:T(8,128)} async-done(((f32[32,5,1,256]{3,0,1,2:T(8,128)}), f32[32,5,16,256]{3,0,1,2:T(8,128)}) %all-gather.5.cloned.1.call-update) | async-done | bytes 2621456 | tf_op jit(solution)/shard_map/all_gather | solution.py:92
  315.9 3.3 copy.25
  319.2 1.5 copy.37
  321.5 1.4 copy.26
  322.9 33.8 %all_to_all.30 = f32[32,4,16,256]{3,1,0,2:T(4,128)S(1)} all-to-all(f32[32,4,16,256]{3,1,0,2:T(4,128)S(1)} %copy.26), channel_id=1, replica_groups=mesh['prow'=16,'pcol'=16] {'pcol'}, dimensions={2} | all-to-all | bytes 4194304 | tf_op jit(solution)/shard_map/all_to_all | solution.py:96
  357.1 1.7 copy-done.1
  358.8 7.0 %fusion.26 = f32[512,1024]{1,0:T(8,128)S(1)} fusion(f32[512,1024]{1,0:T(8,128)S(1)} %bitcast.80, f32[1024,1024]{1,0:T(8,128)S(1)} %bitcast.78), kind=kOutput, calls=%fused_computation.48 | convolution fusion | flops 6442450944 | bytes 8388608 | tf_op jit(solution)/shard_map/dot_general | solution.py:47
  365.8 1.8 fusion.27
  367.6 1.6 pad_maximum_fusion
  370.1 76.6 %reduce-scatter.2.cloned.1.call-done = f32[32,1056]{1,0:T(8,128)} async-done(((f32[512,1056]{1,0:T(8,128)}), f32[32,1056]{1,0:T(8,128)}) %reduce-scatter.2.cloned.1.call-update) | async-done | bytes 135184 | tf_op jit(solution)/shard_map/reduce_scatter | solution.py:38
  448.5 1.6 convolution_add_fusion.1
  (55 shorter events, 15.7 us)
Async XLA Ops:
  11.1 79.2 %all-to-all-start = ((f32[16,32,4,1,256]{4,3,2,1,0:T(1,128)}), f32[16,32,4,1,256]{4,3,2,1,0:T(1,128)S(1)}, u32[]{:S(2)}, u32[]{:S(2)}) async-start(f32[16,32,4,1,256]{4,3,2,1,0:T(1,128)} %broadcast_in_dim.4), calls=%async_computation | async-start | bytes 4194304 | tf_op jit(solution)/shard_map/all_to_all | solution.py:9
  18.5 198.2 %all-gather.3.cloned.1.call-start = ((), (), s32[]{:S(2)}) async-start(), calls=%async_computation.5 | async-start | bytes 2228224 | tf_op jit(solution)/shard_map/all_gather | solution.py:88
  99.7 4.0 copy-start
  169.4 146.5 %all-gather.5.cloned.1.call-start = ((), (), s32[]{:S(2)}) async-start(), calls=%async_computation.6 | async-start | bytes 2785280 | tf_op jit(solution)/shard_map/all_gather | solution.py:92
  206.8 9.2 %copy-start.4 = (f32[32,6,1,256]{3,2,1,0:T(1,128)S(1)}, f32[32,6,1,256]{3,2,1,0:T(1,128)}, u32[]{:S(2)}) copy-start(f32[32,6,1,256]{3,2,1,0:T(1,128)} %param.9) | copy-start | bytes 589828
  216.7 13.7 %copy-start.2 = (f32[512,512]{1,0:T(8,128)}, f32[512,512]{1,0:T(8,128)S(1)}, u32[]{:S(2)}) copy-start(f32[512,512]{1,0:T(8,128)S(1)} %select_maximum_fusion) | copy-start | bytes 3145732
  279.3 167.4 %reduce-scatter.2.cloned.1.call-start = ((), (), s32[]{:S(2)}) async-start(), calls=%async_computation.7 | async-start | bytes 2506752 | tf_op jit(solution)/shard_map/reduce_scatter | solution.py:38
  356.7 2.2 copy-start.1
  358.8 7.0 %copy-start.3 = (f32[32,1024]{1,0:T(8,128)S(1)}, f32[32,1024]{1,0:T(8,128)}, u32[]{:S(2)}) copy-start(f32[32,1024]{1,0:T(8,128)} %reduce_sum.18) | copy-start | bytes 393220
Sparse Core Ops, SparseCore 0:
  169.5 37.7 all-gather.2
  279.4 36.4 all-gather.4
  369.4 77.3 reduce-scatter.1
where the time goes:
time: 464 us; the launch traced here: 457 us
  blocking collectives  137 us (30%)
  waiting for transfers between devices  113 us (24%)
  other arithmetic  103 us (22%)
  matrix products  41.4 us (9%)
  local copies, waits for them, and re-layouts  40.7 us (9%)
  between operations  14.5 us (3%)
  starting transfers between devices  7.6 us (2%)
    all_to_all x2, blocking collectives, sum_at_owner(): lax.all_to_all(parts, axis, split_axis=0, concat_axis=0, tiled=True)  103 us
    reduce_scatter x1, waiting for transfers between devices, in_one_piece(): result = lax.psum_scatter(both, axis, scatter_dimension=dim, tiled=True)  76.6 us
    unnamed x3, other arithmetic  52.1 us
    all_gather x1, waiting for transfers between devices, per_device(): lax.all_gather(kept_cols, 'prow', axis=2, tiled=True).reshape(x_rows, -1)  36.6 us
    all_to_all x1, blocking collectives, per_device(): lax.all_to_all(head_cols.reshape(x_rows, col_blocks, lax.axis_size('pcol'...  33.8 us
    dot_general x6, matrix products, matmul_hi(): jnp.dot(left, right, precision=lax.Precision.HIGHEST, preferred_element_t...  29.3 us
    unnamed x19, local copies, waits for them, and re-layouts  22.7 us
    another operation x2, other arithmetic, invert_diag(): lax.linalg.triangular_solve(diag_bottom, identity, left_side=True, lower=...  20.7 us
  transfers between devices with their start and end apart: 4, of which 2 were waited for; matrix products, arithmetic and copies ran while one was open for 26% of the time, Pallas kernels for 0%

commit v1 on v0

--- a/solution.py
+++ b/solution.py
@@ -93,12 +93,20 @@
     prev_rows = prev_blocks * block_size * lax.axis_size("prow")
     head_cols = widened[:, :prev_rows]
     tail_cols = widened[:, prev_rows : prev_rows + slab_rows]
-    shifted_x = lax.all_to_all(
-        head_cols.reshape(x_rows, col_blocks, lax.axis_size("pcol"), block_size),
-        "pcol",
-        split_axis=2,
-        concat_axis=0,
-        tiled=True,
+    shifted_x = jnp.concatenate(
+        lax.all_to_all(
+            jnp.stack(
+                jnp.split(
+                    head_cols.reshape(x_rows, col_blocks, lax.axis_size("pcol"), block_size),
+                    lax.axis_size("pcol"),
+                    axis=2,
+                )
+            ),
+            "pcol",
+            0,
+            0,
+        ),
+        axis=0,
     )
     shifted_x = shifted_x.reshape(slab_rows, col_width)
     lead_part = matmul_trans(shifted_x, inv_local)

time: 464 us -> 474 us (1.022)
  other arithmetic: 103 us -> 111 us
    all_to_all x0 -> x1, other arithmetic: none -> 8.43 us  [per_device(): lax.all_to_all(jnp.stack(jnp.split(head_cols.reshape(x_rows, col_blocks,...]
    unnamed x19 -> x34, local copies, waits for them, and re-layouts: 22.7 us -> 25.4 us
where the time goes in v1:
time: 474 us; the launch traced here: 467 us
  blocking collectives  137 us (29%)
  waiting for transfers between devices  113 us (24%)
  other arithmetic  111 us (23%)
  local copies, waits for them, and re-layouts  42.5 us (9%)
  matrix products  41.7 us (9%)
  between operations  14.3 us (3%)
  starting transfers between devices  7.6 us (2%)
    all_to_all x2, blocking collectives, sum_at_owner(): lax.all_to_all(parts, axis, split_axis=0, concat_axis=0, tiled=True)  103 us
    reduce_scatter x1, waiting for transfers between devices, in_one_piece(): result = lax.psum_scatter(both, axis, scatter_dimension=dim, tiled=True)  76.6 us
    unnamed x3, other arithmetic  52.1 us
    all_gather x1, waiting for transfers between devices, per_device(): lax.all_gather(kept_cols, 'prow', axis=2, tiled=True).reshape(x_rows, -1)  36.6 us
    all_to_all x1, blocking collectives, per_device(): lax.all_to_all(jnp.stack(jnp.split(head_cols.reshape(x_rows, col_blocks,...  33.6 us
    dot_general x6, matrix products, matmul_hi(): jnp.dot(left, right, precision=lax.Precision.HIGHEST, preferred_element_t...  29.4 us
    unnamed x34, local copies, waits for them, and re-layouts  25.4 us
    another operation x2, other arithmetic, invert_diag(): lax.linalg.triangular_solve(diag_bottom, identity, left_side=True, lower=...  20.7 us
  transfers between devices with their start and end apart: 4, of which 2 were waited for; matrix products, arithmetic and copies ran while one was open for 26% of the time, Pallas kernels for 0%

profile of v1, /device:TPU:2, one launch (start us, length us, event | category | flops | bytes accessed | tf_op | source)
XLA Modules:
  0.0 467.4 jit_solution(13552269376336275357)
XLA Ops:
  8.1 2.9 broadcast_in_dim.4
  11.1 7.5 %all-to-all-start = ((f32[16,32,4,1,256]{4,3,2,1,0:T(1,128)}), f32[16,32,4,1,256]{4,3,2,1,0:T(1,128)S(1)}, u32[]{:S(2)}, u32[]{:S(2)}) async-start(f32[16,32,4,1,256]{4,3,2,1,0:T(1,128)} %broadcast_in_dim.4), calls=%async_computation | async-start | bytes 4194304 | tf_op jit(solution)/shard_map/all_to_all | solution.py:9
  19.8 4.1 while.4
  20.4 1.4 bitcast_dynamic-update-slice_fusion.4
  22.4 1.4 bitcast_dynamic-update-slice_fusion.4
  23.9 19.7 %custom-call.4 = f32[2,128,128]{1,2,0:T(8,128)S(1)} custom-call(f32[2,128,128]{2,1,0:T(8,128)S(1)} %get-tuple-element.18), custom_call_target="InvertDiagBlocksLowerTriangular" | custom-call | tf_op jit(solution)/shard_map/triangular_solve/custom-call.1 | solution.py:61
  43.6 4.0 while.5
  47.6 19.7 %custom-call.5 = f32[2,128,128]{1,2,0:T(8,128)S(1)} custom-call(f32[2,128,128]{2,1,0:T(8,128)S(1)} %get-tuple-element.19), custom_call_target="InvertDiagBlocksLowerTriangular" | custom-call | tf_op jit(solution)/shard_map/triangular_solve/custom-call.1 | solution.py:62
  67.3 14.3 %reduce.1 = f32[4,256,4,256]{3,2,1,0:T(4,128)} reduce(f32[4,1,256,4,1,256]{5,4,3,2,1,0:T(1,128)} %param.7, f32[]{:T(128)} %constant.47), dimensions={1,4}, to_apply=%param.7.reduce_sub_computation | reduce | bytes 8388612 | tf_op args[0]
  81.6 5.2 %copy.25 = f32[128,8,4,256]{3,1,2,0:T(8,128)} copy(f32[128,8,4,256]{3,2,1,0:T(4,128)} %bitcast.142) | data formatting | bytes 8388608
  88.6 1.5 fusion.6
  90.6 7.4 %reduce = f32[16,32,4,256]{3,2,1,0:T(4,128)} reduce(f32[16,32,4,1,256]{4,3,2,1,0:T(1,128)S(1)} %all-to-all-done, f32[]{:T(128)} %constant.47), dimensions={3}, to_apply=%all_to_all.12.reduce_sub_computation | reduce | bytes 4194308 | tf_op jit(solution)/shard_map/all_to_all | solution.py:9
  98.0 2.1 copy.24
  100.0 4.1 fusion.38
  104.1 6.9 %convolution_negate_fusion = f32[512,1024]{1,0:T(8,128)S(1)} fusion(f32[512,1024]{1,0:T(8,128)S(1)} %fusion.38, f32[1024,1024]{1,0:T(8,128)S(1)} %bitcast.137), kind=kOutput, calls=%fused_computation.6 | convolution fusion | flops 6442975232 | bytes 8388608 | tf_op jit(solution)/shard_map/dot_general | solution.py:43
  111.1 58.0 %all_to_all.21 = f32[16,32,1024]{2,1,0:T(8,128)S(1)} all-to-all(f32[16,32,1024]{2,1,0:T(8,128)S(1)} %bitcast.167), channel_id=1, replica_groups=mesh['prow'=16,'pcol'=16] {'prow'}, dimensions={0} | all-to-all | bytes 4194304 | tf_op jit(solution)/shard_map/all_to_all | solution.py:31
  169.9 37.4 %reduce.2 = f32[4,256,6,256]{3,2,1,0:T(8,128)} reduce(f32[4,1,256,6,1,256]{5,4,3,2,1,0:T(1,128)} %param.8, f32[]{:T(128)} %constant.47), dimensions={1,4}, to_apply=%param.8.reduce_sub_computation | reduce | bytes 12582916 | tf_op args[1]
  207.3 9.2 %copy.26 = f32[128,8,6,256]{3,1,2,0:T(8,128)} copy(f32[128,8,6,256]{3,2,1,0:T(8,128)} %bitcast.139) | data formatting | bytes 12582912
  217.2 13.7 %fusion.41 = f32[512,1536]{1,0:T(8,128)S(1)} fusion(f32[512,1024]{1,0:T(8,128)} %all-gather.3.cloned.1.call-done, f32[1024,1536]{1,0:T(8,128)} %bitcast.168), kind=kOutput, calls=%fused_computation.79 | convolution fusion | flops 9663676416 | bytes 11534336 | tf_op jit(solution)/shard_map/dot_general | solution.py:43
  230.9 2.8 convolution_add_fusion
  233.7 45.1 %all_to_all.22 = f32[16,32,1536]{2,1,0:T(8,128)S(1)} all-to-all(f32[16,32,1536]{2,1,0:T(8,128)S(1)} %bitcast.143), channel_id=1, replica_groups=mesh['prow'=16,'pcol'=16] {'pcol'}, dimensions={0} | all-to-all | bytes 6291456 | tf_op jit(solution)/shard_map/all_to_all | solution.py:31
  279.8 36.6 %all-gather.5.cloned.1.call-done = f32[32,5,16,256]{3,0,1,2:T(8,128)} async-done(((f32[32,5,1,256]{3,0,1,2:T(8,128)}), f32[32,5,16,256]{3,0,1,2:T(8,128)}) %all-gather.5.cloned.1.call-update) | async-done | bytes 2621456 | tf_op jit(solution)/shard_map/all_gather | solution.py:92
  316.4 3.3 copy.17
  319.7 1.5 copy.28
  324.3 33.6 %all_to_all.20 = f32[16,32,4,1,256]{4,3,2,1,0:T(1,128)} all-to-all(f32[16,32,4,1,256]{4,3,2,1,0:T(1,128)S(1)} %fusion.9), channel_id=1, replica_groups=mesh['prow'=16,'pcol'=16] {'pcol'}, dimensions={0} | all-to-all | bytes 4194304 | tf_op jit(solution)/shard_map/all_to_all | solution.py:97
  358.0 8.4 %reduce.4 = f32[16,32,4,256]{3,2,1,0:T(4,128)} reduce(f32[16,32,4,1,256]{4,3,2,1,0:T(1,128)} %all_to_all.20, f32[]{:T(128)} %constant.47), dimensions={3}, to_apply=%all_to_all.15.reduce_sub_computation | reduce | bytes 4194308 | tf_op jit(solution)/shard_map/all_to_all | solution.py:97
  366.4 2.2 copy.30
  369.2 7.2 %fusion.42 = f32[512,1024]{1,0:T(8,128)S(1)} fusion(f32[512,1024]{1,0:T(8,128)S(1)} %bitcast.140, f32[1024,1024]{1,0:T(8,128)S(1)} %bitcast.138), kind=kOutput, calls=%fused_computation.80 | convolution fusion | flops 6442450944 | bytes 8388608 | tf_op jit(solution)/shard_map/dot_general | solution.py:47
  376.4 1.8 fusion.43
  378.1 1.6 pad_maximum_fusion
  380.7 76.6 %reduce-scatter.2.cloned.1.call-done = f32[32,1056]{1,0:T(8,128)} async-done(((f32[512,1056]{1,0:T(8,128)}), f32[32,1056]{1,0:T(8,128)}) %reduce-scatter.2.cloned.1.call-update) | async-done | bytes 135184 | tf_op jit(solution)/shard_map/reduce_scatter | solution.py:38
  459.0 1.6 convolution_add_fusion.1
  (71 shorter events, 18.3 us)
Async XLA Ops:
  11.1 79.5 %all-to-all-start = ((f32[16,32,4,1,256]{4,3,2,1,0:T(1,128)}), f32[16,32,4,1,256]{4,3,2,1,0:T(1,128)S(1)}, u32[]{:S(2)}, u32[]{:S(2)}) async-start(f32[16,32,4,1,256]{4,3,2,1,0:T(1,128)} %broadcast_in_dim.4), calls=%async_computation | async-start | bytes 4194304 | tf_op jit(solution)/shard_map/all_to_all | solution.py:9
  18.5 198.7 %all-gather.3.cloned.1.call-start = ((), (), s32[]{:S(2)}) async-start(), calls=%async_computation.5 | async-start | bytes 2228224 | tf_op jit(solution)/shard_map/all_gather | solution.py:88
  100.0 4.1 copy-start
  169.9 146.5 %all-gather.5.cloned.1.call-start = ((), (), s32[]{:S(2)}) async-start(), calls=%async_computation.6 | async-start | bytes 2785280 | tf_op jit(solution)/shard_map/all_gather | solution.py:92
  207.3 9.2 %copy-start.4 = (f32[32,6,1,256]{3,2,1,0:T(1,128)S(1)}, f32[32,6,1,256]{3,2,1,0:T(1,128)}, u32[]{:S(2)}) copy-start(f32[32,6,1,256]{3,2,1,0:T(1,128)} %param.9) | copy-start | bytes 589828
  217.2 13.7 %copy-start.2 = (f32[512,512]{1,0:T(8,128)}, f32[512,512]{1,0:T(8,128)S(1)}, u32[]{:S(2)}) copy-start(f32[512,512]{1,0:T(8,128)S(1)} %select_maximum_fusion) | copy-start | bytes 3145732
  279.8 177.5 %reduce-scatter.2.cloned.1.call-start = ((), (), s32[]{:S(2)}) async-start(), calls=%async_computation.7 | async-start | bytes 2506752 | tf_op jit(solution)/shard_map/reduce_scatter | solution.py:38
  366.4 2.8 copy-start.1
  369.2 7.2 %copy-start.3 = (f32[32,1024]{1,0:T(8,128)S(1)}, f32[32,1024]{1,0:T(8,128)}, u32[]{:S(2)}) copy-start(f32[32,1024]{1,0:T(8,128)} %reduce_sum.18) | copy-start | bytes 393220
Sparse Core Ops, SparseCore 0:
  170.0 37.7 all-gather.2
  279.9 36.4 all-gather.4
  379.9 77.3 reduce-scatter.1
